TPU v7x, 32 devices: a whole 2x2x4 slice. The times are simulated.
32 devices in a mesh: row: 4 (over y, x), col: 8 (over z, core).
Axes of the slice: x: 2, y: 2, z: 4, core: 2. Of those that a mesh axis runs over, the one named last changes fastest.
Arguments:
- integrals: bfloat16 [2400, 2400, 256], P('row', 'col'), may hold values from -6 to 6
- occ_coef: bfloat16 [2400, 96], P('row'), may hold values from -0.125 to 0.125
- virt_coef: bfloat16 [2400, 2304], P('col'), may hold values from -0.125 to 0.125
- pair_index: int32 [256], replicated, may hold values from 0 to 255, each once
Outputs:
- transformed: bfloat16 [96, 2304, 256], P('row', 'col')
Inputs may be any that keep to these rules, and one draw needn't show every extreme that they name: pair_index holds each of 0 to 255 once.
All inputs are finite; a program needn't handle non-finite values.
Results may differ from a plain program's by a relative error of at most 0.0049.
Values may be sent and summed in bfloat16 or wider, within the bound.
A program may use at most 192 MiB of HBM per device.

v0:
```python
import functools

import jax
import jax.numpy as jnp
from jax import lax
from jax.experimental import pallas as pl
from jax.experimental.pallas import tpu as pltpu
from jax.sharding import PartitionSpec as P

MESH = pl.DeviceIdType.MESH
F32 = jnp.float32
BF16 = jnp.bfloat16

LANES = 128
GROUP = 8
STEP = 16
SIDES = 2
LAG_A = 2
LAG_B = 3
LAG_S = 2


def kernel(
    dims,
    x_hbm, occ_ref, vt_hbm, out_hbm,
    ibuf, part, ra, rb, half, vr, qs, qr, fsum,
    i_sem, a_send, a_recv, b_send, b_recv, own_send, own_recv, fw_send, fw_recv,
    q_send, q_recv, o_send, o_recv, l_sem, v_send, v_recv, v_loc,
):
    nus, steps, blocks, granules = dims
    padded = steps * STEP
    per_block = granules * steps
    total = blocks * per_block
    pairs = GROUP // 2
    units = GROUP
    rows_step = STEP * GROUP

    row, col = lax.axis_index("row"), lax.axis_index("col")
    y, x = row // 2, row % 2
    z, c = col // 2, col % 2
    xn, yn, dg = row + 1 - 2 * x, row + 2 - 4 * y, 3 - row
    inner_i = (z % 2 + z // 2) % 2
    inner = inner_i == 1
    outer = inner_i == 0
    zp = z + 1 - 2 * (z % 2)
    zm = 3 - z
    zmp = zm + 1 - 2 * (zm % 2)
    core_col = col + 1 - 2 * c
    pair_col = zp * 2 + c
    mid_col = zm * 2 + c
    q = (z % 2) * 2 + c
    qp = (z % 2) * 2 + 1 - c
    qo = (zp % 2) * 2 + c
    far = (1 - z // 2) * 2
    near = (z // 2) * 2

    def rcopy(src, dst, ssem, rsem, dev):
        return pltpu.make_async_remote_copy(
            src_ref=src, dst_ref=dst, send_sem=ssem, recv_sem=rsem, device_id=dev, device_id_type=MESH
        )

    barrier = pltpu.get_barrier_semaphore()
    peers = (
        (xn, col), (yn, col), (row, core_col), (row, pair_col), (row, zp * 2 + 1 - c), (row, mid_col),
    )
    for dev in peers:
        pl.semaphore_signal(barrier, inc=1, device_id=dev, device_id_type=MESH)
    pl.semaphore_wait(barrier, len(peers))

    def place(s):
        h = s // per_block
        rem = s % per_block
        return h, rem // steps, rem % steps

    def rows_of(k):
        return pl.ds(pl.multiple_of(k * rows_step, rows_step), rows_step)

    def chunk(j):
        h, k = j // steps, j % steps
        base = jnp.minimum(k * STEP, nus - STEP)
        return pltpu.make_async_copy(
            x_hbm.at[pl.ds(base, STEP), :, pl.ds(pl.multiple_of(h * LANES, LANES), LANES)],
            ibuf.at[j % 2],
            i_sem.at[j % 2],
        )

    def turn(s):
        par = s % 2
        return xn + par * (yn - xn), yn + par * (xn - yn)

    def a_copy(s, j):
        h, g, k = place(s)
        n1, _ = turn(s)
        r = rows_of(k)
        block = dg if j == 0 else n1
        return rcopy(part.at[h, g, block, r], ra.at[h, g, j, r], a_send.at[s, j], a_recv.at[s, j], (n1, col))

    def b_copy(s):
        h, g, k = place(s)
        _, n2 = turn(s)
        r = rows_of(k)
        return rcopy(part.at[h, g, n2, r], rb.at[h, g, r], b_send.at[s], b_recv.at[s], (n2, col))

    def half_at(s, quarter):
        h, g, k = place(s)
        return half.at[
            h, pl.ds(g * GROUP, GROUP), pl.ds(pl.multiple_of(quarter * padded + k * STEP, STEP), STEP), :
        ]

    own_col = inner_i * core_col + (1 - inner_i) * pair_col

    def own_copy(s):
        ref = half_at(s, q)
        return rcopy(ref, ref, own_send.at[s], own_recv.at[1 - inner_i, s], (row, own_col))

    def own_arrival(s, kind, quarter):
        ref = half_at(s, quarter)
        return rcopy(ref, ref, own_send.at[s], own_recv.at[kind, s], (row, core_col))

    def fw_copy(s):
        ref = half_at(s, qo)
        return rcopy(ref, ref, fw_send.at[s], fw_recv.at[s], (row, core_col))

    def fw_arrival(s):
        ref = half_at(s, (zp % 2) * 2 + 1 - c)
        return rcopy(ref, ref, fw_send.at[s], fw_recv.at[s], (row, core_col))

    def v_core():
        return rcopy(vt_hbm.at[1 - c], vr.at[q], v_send.at[0], v_recv.at[q, 0], (row, core_col))

    def v_core_arrival():
        return rcopy(vt_hbm.at[1 - c], vr.at[qp], v_send.at[0], v_recv.at[qp, 0], (row, core_col))

    def v_local():
        return pltpu.make_async_copy(vt_hbm.at[c], vr.at[q], v_loc)

    def v_pair(core, side):
        start = far if side == 0 else near
        return rcopy(
            vt_hbm.at[core, pl.ds(start, 2)], vr.at[q, pl.ds(start, 2)],
            v_send.at[core * 2 + side], v_recv.at[q, side], (row, zp * 2 + core),
        )

    def v_pair_arrival(core, side):
        start = far if side == 0 else near
        src = (zp % 2) * 2 + core
        return rcopy(
            vt_hbm.at[core, pl.ds(start, 2)], vr.at[src, pl.ds(start, 2)],
            v_send.at[core * 2 + side], v_recv.at[src, side], (row, pair_col),
        )

    def unit(n):
        gr, m = n // units, n % units
        return gr // granules, gr % granules, m // 2, m % 2

    def product(h, g, pair, zb):
        acc = None
        i0 = g * GROUP + pair * 2
        for quarter in range(4):
            r = pl.ds(quarter * padded, padded)
            w = jnp.concatenate([half[h, i0, r, :], half[h, i0 + 1, r, :]], axis=1)
            term = jnp.dot(vr[quarter, zb], w, preferred_element_type=F32)
            acc = term if acc is None else acc + term
        return acc

    def q_copy(n):
        h, g, pair, b = unit(n)
        pi = g * pairs + pair
        return rcopy(qs.at[h, pi, b], qr.at[h, pi, b], q_send.at[n], q_recv.at[n], (row, mid_col))

    def out_at(n):
        h, g, pair, _ = unit(n)
        return out_hbm.at[pl.ds(g * GROUP + pair * 2, 2), :, pl.ds(pl.multiple_of(h * LANES, LANES), LANES)]

    def o_local(n):
        h, g, pair, _ = unit(n)
        return pltpu.make_async_copy(qr.at[h, g * pairs + pair, 0], out_at(n), l_sem.at[n // 2])

    def o_copy(n):
        h, g, pair, _ = unit(n)
        return rcopy(
            qr.at[h, g * pairs + pair, 1], out_at(n), o_send.at[n // 2], o_recv.at[n // 2], (row, pair_col)
        )

    def q_unit(n):
        h, g, pair, b = unit(n)
        pi = g * pairs + pair
        acc = product(h, g, pair, zm + b * (zmp - zm))
        qs[h, pi, b, 0] = acc[:, :LANES].astype(BF16)
        qs[h, pi, b, 1] = acc[:, LANES:].astype(BF16)
        q_copy(n).start()

    def s_unit(n):
        h, g, pair, b = unit(n)
        pi = g * pairs + pair
        q_copy(n).wait_recv()
        acc = product(h, g, pair, z + b * (zp - z))
        qr[h, pi, b, 0] = (acc[:, :LANES] + qr[h, pi, b, 0].astype(F32)).astype(BF16)
        qr[h, pi, b, 1] = (acc[:, LANES:] + qr[h, pi, b, 1].astype(F32)).astype(BF16)

        @pl.when(b == 0)
        def _():
            o_local(n).start()

        @pl.when(b == 1)
        def _():
            o_copy(n).start()

    chunk(0).start()

    @pl.when(inner)
    def _():
        v_local().start()
        v_core().start()

    @pl.when(outer)
    def _():
        v_pair(0, 0).start()
        v_pair(1, 0).start()

    n_chunks = blocks * steps

    def compute(j):
        h, k = j // steps, j % steps
        slot = j % 2
        chunk(j).wait()

        @pl.when(j + 1 < n_chunks)
        def _():
            chunk(j + 1).start()

        def couple(u, carry):
            w = jnp.concatenate([ibuf[slot, 2 * u], ibuf[slot, 2 * u + 1]], axis=1)
            r = jnp.dot(occ_ref[...], w, preferred_element_type=F32)
            cells = r.shape[0] // GROUP
            r0 = r[:, :LANES].reshape(cells, 1, GROUP, LANES)
            r1 = r[:, LANES:].reshape(cells, 1, GROUP, LANES)
            v = jnp.concatenate([r0, r1], axis=1).reshape(granules, 4, 2 * GROUP, LANES).astype(BF16)
            at = pl.multiple_of(k * rows_step + u * 2 * GROUP, 2 * GROUP)
            part[h, :, :, pl.ds(at, 2 * GROUP), :] = v
            return carry

        lax.fori_loop(0, STEP // 2, couple, 0, unroll=2)

    lag_f = LAG_B + 1
    lag_q = LAG_B + 2 + steps

    def iteration(t, carry):
        @pl.when(t < n_chunks)
        def _():
            compute(t)

        @pl.when(t < total)
        def _():
            for j in range(2):
                a_copy(t, j).start()

        s1 = t - LAG_A

        @pl.when((s1 >= 0) & (s1 < total))
        def _():
            h, g, k = place(s1)
            _, n2 = turn(s1)
            r = rows_of(k)
            a_copy(s1, 0).wait_recv()
            part[h, g, n2, r, :] = (part[h, g, n2, r, :].astype(F32) + ra[h, g, 0, r, :].astype(F32)).astype(BF16)
            b_copy(s1).start()

        s2 = t - LAG_B

        @pl.when((s2 >= 0) & (s2 < total))
        def _():
            h, g, k = place(s2)
            r = rows_of(k)
            a_copy(s2, 1).wait_recv()
            b_copy(s2).wait_recv()
            fsum[...] = (
                part[h, g, row, r, :].astype(F32) + ra[h, g, 1, r, :].astype(F32) + rb[h, g, r, :].astype(F32)
            )
            at = pl.multiple_of(q * padded + k * STEP, STEP)
            for i in range(GROUP):
                half[h, g * GROUP + i, pl.ds(at, STEP), :] = fsum[pl.ds(i, STEP, stride=GROUP), :].astype(BF16)
            own_copy(s2).start()

        @pl.when(outer & (t == steps + LAG_B))
        def _():
            v_pair(0, 1).start()
            v_pair(1, 1).start()

        tf = t - lag_f
        gf, uf = tf // steps, tf % steps

        @pl.when(inner & (tf >= 0) & (tf < total))
        def _():
            for j in range(2):
                kf = 2 * uf - (steps - 1) + j

                @pl.when((kf >= 0) & (kf < steps))
                def _():
                    s = gf * steps + kf
                    own_arrival(s, 1, qo).wait_recv()
                    fw_copy(s).start()

        tq = t - lag_q
        gq, uq = tq // steps, tq % steps

        @pl.when(inner & (tq == 0))
        def _():
            v_local().wait()
            v_core_arrival().wait_recv()
            v_pair_arrival(0, 0).wait_recv()
            v_pair_arrival(1, 0).wait_recv()

        @pl.when(inner & (tq >= 0) & (tq < total) & (uq == 0))
        def _():
            def arrivals(k, inner_carry):
                s = gq * steps + k
                own_arrival(s, 0, qp).wait_recv()
                fw_arrival(s).wait_recv()
                return inner_carry

            lax.fori_loop(0, steps, arrivals, 0)

        @pl.when(inner & (tq >= 0) & (tq < total) & (uq < units))
        def _():
            q_unit(gq * units + uq)

        gs = gq - LAG_S

        @pl.when(inner & (tq >= 0) & (gs == 0) & (uq == units))
        def _():
            v_pair_arrival(0, 1).wait_recv()
            v_pair_arrival(1, 1).wait_recv()

        @pl.when(inner & (tq >= 0) & (tq < total) & (gs >= 0) & (uq >= units) & (uq < 2 * units))
        def _():
            s_unit(gs * units + uq - units)

        return carry

    lax.fori_loop(0, total + LAG_B + 2 + units, iteration, 0)

    n_units = blocks * granules * units
    done_units = (blocks * granules - 1 - LAG_S) * units

    @pl.when(inner)
    def _():
        def finish(n, carry):
            s_unit(n)
            return carry

        lax.fori_loop(done_units, n_units, finish, 0)

        def drain(s, carry):
            fw_copy(s).wait_send()
            return carry

        lax.fori_loop(0, total, drain, 0)

        def drain_units(n, carry):
            q_copy(n).wait_send()

            @pl.when(n % 2 == 0)
            def _():
                o_local(n).wait()
                o_copy(n).wait_send()

            return carry

        lax.fori_loop(0, n_units, drain_units, 0)
        v_core().wait_send()

    @pl.when(outer)
    def _():
        def outputs(n, carry):
            o_copy(2 * n).wait_recv()
            return carry

        lax.fori_loop(0, n_units // 2, outputs, 0)
        for core in range(2):
            for side in range(2):
                v_pair(core, side).wait_send()

    def drain_all(s, carry):
        for j in range(2):
            a_copy(s, j).wait_send()
        b_copy(s).wait_send()
        own_copy(s).wait_send()
        return carry

    lax.fori_loop(0, total, drain_all, 0)


def fused(integrals, occ_coef, virt_coef, pair_index):
    rows, cols = lax.axis_size("row"), lax.axis_size("col")
    mus, nus, n_pairs = integrals.shape
    occ = occ_coef.shape[1]
    virt = virt_coef.shape[1]
    depth, width = occ // rows, virt // cols
    granules, blocks = depth // GROUP, n_pairs // LANES
    steps = -(-nus // STEP)
    padded = steps * STEP
    tail = padded - STEP
    total = blocks * granules * steps
    n_units = blocks * granules * GROUP
    halves = GROUP // 2 * granules

    flipped = jnp.transpose(integrals, (1, 0, 2))
    occ_rows = occ_coef.reshape(mus, rows, granules, GROUP).transpose(2, 1, 3, 0).reshape(occ, mus)
    spread = jnp.concatenate(
        [virt_coef[:tail], jnp.zeros((padded - nus, virt), BF16), virt_coef[tail:]], axis=0
    )
    columns = spread.reshape(padded, cols // 2, 2, width).transpose(2, 1, 3, 0)

    dma = pltpu.SemaphoreType.DMA
    r = padded * GROUP
    slab = pl.pallas_call(
        functools.partial(kernel, (nus, steps, blocks, granules)),
        out_shape=jax.ShapeDtypeStruct((depth, width, n_pairs), BF16),
        in_specs=[
            pl.BlockSpec(memory_space=pl.ANY),
            pl.BlockSpec(memory_space=pltpu.VMEM),
            pl.BlockSpec(memory_space=pl.ANY),
        ],
        out_specs=pl.BlockSpec(memory_space=pl.ANY),
        scratch_shapes=[
            pltpu.VMEM((2, STEP, mus, LANES), BF16),
            pltpu.VMEM((blocks, granules, rows, r, LANES), BF16),
            pltpu.VMEM((blocks, granules, 2, r, LANES), BF16),
            pltpu.VMEM((blocks, granules, r, LANES), BF16),
            pltpu.VMEM((blocks, depth, 4 * padded, LANES), BF16),
            pltpu.VMEM((4, cols // 2, width, padded), BF16),
            pltpu.VMEM((blocks, halves, 2, 2, width, LANES), BF16),
            pltpu.VMEM((blocks, halves, 2, 2, width, LANES), BF16),
            pltpu.VMEM((STEP * GROUP, LANES), F32),
            dma((2,)),
            dma((total, 2)), dma((total, 2)),
            dma((total,)), dma((total,)),
            dma((total,)), dma((2, total)),
            dma((total,)), dma((total,)),
            dma((n_units,)), dma((n_units,)),
            dma((n_units // 2,)), dma((n_units // 2,)), dma((n_units // 2,)),
            dma((4,)), dma((4, 2)), dma,
        ],
        compiler_params=pltpu.CompilerParams(
            collective_id=0, has_side_effects=True, vmem_limit_bytes=67043328
        ),
        name="half_transform",
    )(flipped, occ_rows, columns)
    chosen = (lax.broadcasted_iota(jnp.int32, (n_pairs, n_pairs), 0) == pair_index[None, :]).astype(BF16)
    return jnp.einsum("iap,pk->iak", slab, chosen, preferred_element_type=F32).astype(BF16)


CHUNKS = 2


def plain(integrals, occ_coef, virt_coef, pair_index):
    rows = lax.axis_size("row")
    mus, occ = occ_coef.shape
    virt_all = lax.all_gather(virt_coef, "col", axis=0, tiled=True)
    depth = occ // rows // CHUNKS
    occ_parts = occ_coef.reshape(mus, rows, CHUNKS, depth)
    outs = []
    for c in range(CHUNKS):
        part = jnp.einsum(
            "mri,mnp->rinp", occ_parts[:, :, c], integrals, preferred_element_type=F32
        ).astype(BF16)
        parts = lax.all_to_all(part, "row", split_axis=0, concat_axis=0, tiled=True)
        half = jnp.sum(parts.astype(F32), axis=0).astype(BF16)
        spread = lax.all_to_all(half, "col", split_axis=2, concat_axis=1, tiled=True)
        slab = jnp.einsum(
            "inp,na->iap", spread, virt_all, preferred_element_type=F32
        ).astype(BF16)
        outs.append(lax.all_to_all(slab, "col", split_axis=1, concat_axis=2, tiled=True))
    return jnp.take(jnp.concatenate(outs, axis=0), pair_index, axis=2)


def local(integrals, occ_coef, virt_coef, pair_index):
    rows, cols = lax.axis_size("row"), lax.axis_size("col")
    fits = (
        rows == SIDES**2
        and cols == SIDES**3
        and integrals.shape[1] >= STEP
        and integrals.shape[2] % LANES == 0
        and occ_coef.shape[1] % (rows * GROUP) == 0
        and virt_coef.shape[1] % (cols * 16) == 0
    )
    form = fused if fits else plain
    return form(integrals, occ_coef, virt_coef, pair_index)


def solution(mesh):
    return jax.shard_map(
        local,
        mesh=mesh,
        in_specs=(P("row", "col", None), P("row", None), P("col", None), P()),
        out_specs=P("row", "col", None),
        check_vma=False,
    )
```

profile of v0, /device:TPU:0, one launch (start us, length us, event | category | flops | bytes accessed | tf_op | source)
XLA Modules:
  0.0 309.4 jit_solution(4447869064998817052)
XLA Ops:
  0.0 0.0 slice-start
  0.0 0.0 slice-start.1
  0.0 0.1 pad.1.clone
  0.1 1.7 copy.6
  1.7 0.0 slice-done
  1.7 0.0 slice-done.1
  1.7 0.3 pad_maximum_fusion
  2.1 2.9 reshape.12
  5.0 5.3 %copy.7 = bf16[304,4,2,288]{0,3,1,2:T(8,128)(2,1)} copy(bf16[304,4,2,288]{3,2,1,0:T(2,128)(2,1)S(1)} %reshape.12) | data formatting | bytes 2801664 | tf_op jit(solution)/shard_map/reshape | solution.py:413
  10.3 294.3 %half_transform.1 = bf16[24,288,256]{2,1,0:T(8,128)(2,1)} custom-call(bf16[300,600,256]{2,1,0:T(8,128)(2,1)} %bitcast.x_hbm, bf16[96,600]{1,0:T(8,128)(2,1)} %bitcast.11, bf16[2,4,288,304]{3,2,1,0:T(8,128)(2,1)} %bitcast.10), custom_call_target="tpu_custom_call" | custom-call | tf_op jit(solution)/shard_map/half_transform/pallas_call | solution.py:417
  304.5 4.9 %convolution_convert_fusion = bf16[24,288,256]{2,1,0:T(8,128)(2,1)} fusion(bf16[24,288,256]{2,1,0:T(8,128)(2,1)} %half_transform.1, s32[256]{0:T(256)} %param.7), kind=kOutput, calls=%fused_computation | convolution fusion | flops 907804672 | bytes 7078912 | tf_op jit(solution)/shard_map/iap,pk->iak/dot_general | solution.py:451
  (1 shorter events, 0.0 us)
Async XLA Ops:
  0.0 1.7 slice-start
  0.0 1.7 slice-start.1
where the time goes:
time: 311 us; the launch traced here: 309 us
  Pallas kernels  294 us (95%)
  local copies, waits for them, and re-layouts  9.92 us (3%)
  matrix products  4.9 us (2%)
    pallas_call x1, Pallas kernels, fused(): pl.pallas_call(functools.partial(kernel, (nus, steps, blocks, granules)),...  294 us
    reshape x2, local copies, waits for them, and re-layouts, fused(): columns = spread.reshape(padded, cols // 2, 2, width).transpose(2, 1, 3, 0)  8.18 us

commit v1 on v0

--- a/solution.py
+++ b/solution.py
@@ -15,9 +15,11 @@
 GROUP = 8
 STEP = 16
 SIDES = 2
-LAG_A = 2
-LAG_B = 3
-LAG_S = 2
+LAG_A = 4
+LAG_B = 8
+LAG_S = 1
+RING = 20
+BATCH = 4
 
 
 def kernel(
@@ -32,7 +34,7 @@
     per_block = granules * steps
     total = blocks * per_block
     pairs = GROUP // 2
-    units = GROUP
+    units = pairs
     rows_step = STEP * GROUP
 
     row, col = lax.axis_index("row"), lax.axis_index("col")
@@ -44,7 +46,6 @@
     outer = inner_i == 0
     zp = z + 1 - 2 * (z % 2)
     zm = 3 - z
-    zmp = zm + 1 - 2 * (zm % 2)
     core_col = col + 1 - 2 * c
     pair_col = zp * 2 + c
     mid_col = zm * 2 + c
@@ -93,51 +94,60 @@
         n1, _ = turn(s)
         r = rows_of(k)
         block = dg if j == 0 else n1
-        return rcopy(part.at[h, g, block, r], ra.at[h, g, j, r], a_send.at[s, j], a_recv.at[s, j], (n1, col))
+        return rcopy(part.at[h, g, block, r], ra.at[h, g, j, r], a_send.at[j], a_recv.at[s % RING, j], (n1, col))
 
     def b_copy(s):
         h, g, k = place(s)
         _, n2 = turn(s)
         r = rows_of(k)
-        return rcopy(part.at[h, g, n2, r], rb.at[h, g, r], b_send.at[s], b_recv.at[s], (n2, col))
-
-    def half_at(s, quarter):
-        h, g, k = place(s)
-        return half.at[
-            h, pl.ds(g * GROUP, GROUP), pl.ds(pl.multiple_of(quarter * padded + k * STEP, STEP), STEP), :
-        ]
+        return rcopy(part.at[h, g, n2, r], rb.at[h, g, r], b_send, b_recv.at[s % RING], (n2, col))
+
+    def half_at(gr, first, count, quarter):
+        h, g = gr // granules, gr % granules
+        at = pl.multiple_of(quarter * padded + first * STEP, STEP)
+        return half.at[h, pl.ds(g * GROUP, GROUP), pl.ds(at, count * STEP), :]
 
     own_col = inner_i * core_col + (1 - inner_i) * pair_col
+    batches = [(b, min(BATCH, steps - b)) for b in range(0, steps, BATCH)]
 
     def own_copy(s):
-        ref = half_at(s, q)
-        return rcopy(ref, ref, own_send.at[s], own_recv.at[1 - inner_i, s], (row, own_col))
-
-    def own_arrival(s, kind, quarter):
-        ref = half_at(s, quarter)
-        return rcopy(ref, ref, own_send.at[s], own_recv.at[kind, s], (row, core_col))
-
-    def fw_copy(s):
-        ref = half_at(s, qo)
-        return rcopy(ref, ref, fw_send.at[s], fw_recv.at[s], (row, core_col))
-
-    def fw_arrival(s):
-        ref = half_at(s, (zp % 2) * 2 + 1 - c)
-        return rcopy(ref, ref, fw_send.at[s], fw_recv.at[s], (row, core_col))
+        gr, k = s // steps, s % steps
+        ref = half_at(gr, k, 1, q)
+        slot = (1 - inner_i) * (1 + k // BATCH)
+        return rcopy(ref, ref, own_send, own_recv.at[gr, slot], (row, own_col))
+
+    def own_batch(gr, b):
+        ref = half_at(gr, *batches[b], qo)
+        return rcopy(ref, ref, own_send, own_recv.at[gr, 1 + b], (row, core_col))
+
+    def own_arrival(gr):
+        ref = half_at(gr, 0, steps, qp)
+        return rcopy(ref, ref, own_send, own_recv.at[gr, 0], (row, core_col))
+
+    def fw_copy(gr, b):
+        ref = half_at(gr, *batches[b], qo)
+        return rcopy(ref, ref, fw_send, fw_recv.at[gr], (row, core_col))
+
+    def fw_arrival(gr):
+        ref = half_at(gr, 0, steps, (zp % 2) * 2 + 1 - c)
+        return rcopy(ref, ref, fw_send, fw_recv.at[gr], (row, core_col))
+
+    def quarter_of(which):
+        return half.at[:, :, pl.ds(pl.multiple_of(which * padded, STEP), padded), :]
 
     def v_core():
-        return rcopy(vt_hbm.at[1 - c], vr.at[q], v_send.at[0], v_recv.at[q, 0], (row, core_col))
+        return rcopy(vt_hbm.at[:, 1 - c], vr.at[q], v_send.at[0], v_recv.at[q, 0], (row, core_col))
 
     def v_core_arrival():
-        return rcopy(vt_hbm.at[1 - c], vr.at[qp], v_send.at[0], v_recv.at[qp, 0], (row, core_col))
+        return rcopy(vt_hbm.at[:, 1 - c], vr.at[qp], v_send.at[0], v_recv.at[qp, 0], (row, core_col))
 
     def v_local():
-        return pltpu.make_async_copy(vt_hbm.at[c], vr.at[q], v_loc)
+        return pltpu.make_async_copy(vt_hbm.at[:, c], vr.at[q], v_loc)
 
     def v_pair(core, side):
         start = far if side == 0 else near
         return rcopy(
-            vt_hbm.at[core, pl.ds(start, 2)], vr.at[q, pl.ds(start, 2)],
+            vt_hbm.at[pl.ds(start, 2), core], vr.at[q, pl.ds(start, 2)],
             v_send.at[core * 2 + side], v_recv.at[q, side], (row, zp * 2 + core),
         )
 
@@ -145,66 +155,60 @@
         start = far if side == 0 else near
         src = (zp % 2) * 2 + core
         return rcopy(
-            vt_hbm.at[core, pl.ds(start, 2)], vr.at[src, pl.ds(start, 2)],
+            vt_hbm.at[pl.ds(start, 2), core], vr.at[src, pl.ds(start, 2)],
             v_send.at[core * 2 + side], v_recv.at[src, side], (row, pair_col),
         )
 
     def unit(n):
-        gr, m = n // units, n % units
-        return gr // granules, gr % granules, m // 2, m % 2
-
-    def product(h, g, pair, zb):
+        gr, pair = n // units, n % units
+        return gr // granules, gr % granules, pair
+
+    def product(h, g, pair, start):
         acc = None
         i0 = g * GROUP + pair * 2
         for quarter in range(4):
             r = pl.ds(quarter * padded, padded)
             w = jnp.concatenate([half[h, i0, r, :], half[h, i0 + 1, r, :]], axis=1)
-            term = jnp.dot(vr[quarter, zb], w, preferred_element_type=F32)
+            coef = vr[quarter, pl.ds(start, 2)]
+            term = jnp.dot(coef.reshape(-1, padded), w, preferred_element_type=F32)
             acc = term if acc is None else acc + term
-        return acc
+        return acc.reshape(2, -1, 2 * LANES)
 
     def q_copy(n):
-        h, g, pair, b = unit(n)
+        h, g, pair = unit(n)
         pi = g * pairs + pair
-        return rcopy(qs.at[h, pi, b], qr.at[h, pi, b], q_send.at[n], q_recv.at[n], (row, mid_col))
+        return rcopy(qs.at[h, pi], qr.at[h, pi], q_send, q_recv.at[n], (row, mid_col))
 
     def out_at(n):
-        h, g, pair, _ = unit(n)
+        h, g, pair = unit(n)
         return out_hbm.at[pl.ds(g * GROUP + pair * 2, 2), :, pl.ds(pl.multiple_of(h * LANES, LANES), LANES)]
 
     def o_local(n):
-        h, g, pair, _ = unit(n)
-        return pltpu.make_async_copy(qr.at[h, g * pairs + pair, 0], out_at(n), l_sem.at[n // 2])
+        h, g, pair = unit(n)
+        return pltpu.make_async_copy(qr.at[h, g * pairs + pair, z % 2], out_at(n), l_sem)
 
     def o_copy(n):
-        h, g, pair, _ = unit(n)
-        return rcopy(
-            qr.at[h, g * pairs + pair, 1], out_at(n), o_send.at[n // 2], o_recv.at[n // 2], (row, pair_col)
-        )
+        h, g, pair = unit(n)
+        return rcopy(qr.at[h, g * pairs + pair, zp % 2], out_at(n), o_send, o_recv, (row, pair_col))
 
     def q_unit(n):
-        h, g, pair, b = unit(n)
+        h, g, pair = unit(n)
         pi = g * pairs + pair
-        acc = product(h, g, pair, zm + b * (zmp - zm))
-        qs[h, pi, b, 0] = acc[:, :LANES].astype(BF16)
-        qs[h, pi, b, 1] = acc[:, LANES:].astype(BF16)
+        acc = product(h, g, pair, far)
+        for j in range(2):
+            qs[h, pi, :, j] = acc[:, :, j * LANES:(j + 1) * LANES].astype(BF16)
         q_copy(n).start()
 
     def s_unit(n):
-        h, g, pair, b = unit(n)
+        h, g, pair = unit(n)
         pi = g * pairs + pair
         q_copy(n).wait_recv()
-        acc = product(h, g, pair, z + b * (zp - z))
-        qr[h, pi, b, 0] = (acc[:, :LANES] + qr[h, pi, b, 0].astype(F32)).astype(BF16)
-        qr[h, pi, b, 1] = (acc[:, LANES:] + qr[h, pi, b, 1].astype(F32)).astype(BF16)
-
-        @pl.when(b == 0)
-        def _():
-            o_local(n).start()
-
-        @pl.when(b == 1)
-        def _():
-            o_copy(n).start()
+        acc = product(h, g, pair, near)
+        for j in range(2):
+            total_j = acc[:, :, j * LANES:(j + 1) * LANES] + qr[h, pi, :, j].astype(F32)
+            qr[h, pi, :, j] = total_j.astype(BF16)
+        o_copy(n).start()
+        o_local(n).start()
 
     chunk(0).start()
 
@@ -223,11 +227,12 @@
     def compute(j):
         h, k = j // steps, j % steps
         slot = j % 2
+
+        @pl.when(j + 1 < n_chunks)
+        def _():
+            chunk(j + 1).start()
+
         chunk(j).wait()
-
-        @pl.when(j + 1 < n_chunks)
-        def _():
-            chunk(j + 1).start()
 
         def couple(u, carry):
             w = jnp.concatenate([ibuf[slot, 2 * u], ibuf[slot, 2 * u + 1]], axis=1)
@@ -235,20 +240,27 @@
             cells = r.shape[0] // GROUP
             r0 = r[:, :LANES].reshape(cells, 1, GROUP, LANES)
             r1 = r[:, LANES:].reshape(cells, 1, GROUP, LANES)
-            v = jnp.concatenate([r0, r1], axis=1).reshape(granules, 4, 2 * GROUP, LANES).astype(BF16)
+            v = jnp.concatenate([r0, r1], axis=1).reshape(4, granules, 2 * GROUP, LANES).astype(BF16)
             at = pl.multiple_of(k * rows_step + u * 2 * GROUP, 2 * GROUP)
-            part[h, :, :, pl.ds(at, 2 * GROUP), :] = v
+            for o in range(4):
+                part[h, :, o, pl.ds(at, 2 * GROUP), :] = v[o]
             return carry
 
-        lax.fori_loop(0, STEP // 2, couple, 0, unroll=2)
-
-    lag_f = LAG_B + 1
-    lag_q = LAG_B + 2 + steps
+        lax.fori_loop(0, STEP // 2, couple, 0, unroll=STEP // 2)
+
+    s_every = max((steps - 1) // (2 * units), 1)
+    s_first = steps - 1 - s_every * (units - 1)
+    lag_f = LAG_B + 3
+    lag_q = LAG_B + 4 + steps
+    spread = max((per_block + steps - 1 - lag_q) // (steps - 1), 1)
 
     def iteration(t, carry):
-        @pl.when(t < n_chunks)
-        def _():
-            compute(t)
+        past = t - lag_q
+        ready = jnp.where(t < steps, t, steps + past // spread)
+
+        @pl.when((t < steps) | ((past >= 0) & (past % spread == 0) & (ready < n_chunks)))
+        def _():
+            compute(ready)
 
         @pl.when(t < total)
         def _():
@@ -292,14 +304,12 @@
 
         @pl.when(inner & (tf >= 0) & (tf < total))
         def _():
-            for j in range(2):
-                kf = 2 * uf - (steps - 1) + j
-
-                @pl.when((kf >= 0) & (kf < steps))
+            for b in range(len(batches)):
+
+                @pl.when(uf == steps - 1 - 2 * (len(batches) - 1 - b))
                 def _():
-                    s = gf * steps + kf
-                    own_arrival(s, 1, qo).wait_recv()
-                    fw_copy(s).start()
+                    own_batch(gf, b).wait_recv()
+                    fw_copy(gf, b).start()
 
         tq = t - lag_q
         gq, uq = tq // steps, tq % steps
@@ -313,13 +323,8 @@
 
         @pl.when(inner & (tq >= 0) & (tq < total) & (uq == 0))
         def _():
-            def arrivals(k, inner_carry):
-                s = gq * steps + k
-                own_arrival(s, 0, qp).wait_recv()
-                fw_arrival(s).wait_recv()
-                return inner_carry
-
-            lax.fori_loop(0, steps, arrivals, 0)
+            own_arrival(gq).wait_recv()
+            fw_arrival(gq).wait_recv()
 
         @pl.when(inner & (tq >= 0) & (tq < total) & (uq < units))
         def _():
@@ -327,18 +332,20 @@
 
         gs = gq - LAG_S
 
-        @pl.when(inner & (tq >= 0) & (gs == 0) & (uq == units))
+        @pl.when(inner & (tq >= 0) & (gs == 0) & (uq == s_first))
         def _():
             v_pair_arrival(0, 1).wait_recv()
             v_pair_arrival(1, 1).wait_recv()
 
-        @pl.when(inner & (tq >= 0) & (tq < total) & (gs >= 0) & (uq >= units) & (uq < 2 * units))
-        def _():
-            s_unit(gs * units + uq - units)
+        us = uq - s_first
+
+        @pl.when(inner & (tq >= 0) & (tq < total) & (gs >= 0) & (us >= 0) & (us % s_every == 0) & (us // s_every < units))
+        def _():
+            s_unit(gs * units + us // s_every)
 
         return carry
 
-    lax.fori_loop(0, total + LAG_B + 2 + units, iteration, 0)
+    lax.fori_loop(0, total + lag_q - steps + units, iteration, 0)
 
     n_units = blocks * granules * units
     done_units = (blocks * granules - 1 - LAG_S) * units
@@ -351,44 +358,23 @@
 
         lax.fori_loop(done_units, n_units, finish, 0)
 
-        def drain(s, carry):
-            fw_copy(s).wait_send()
-            return carry
-
-        lax.fori_loop(0, total, drain, 0)
-
-        def drain_units(n, carry):
-            q_copy(n).wait_send()
-
-            @pl.when(n % 2 == 0)
-            def _():
-                o_local(n).wait()
-                o_copy(n).wait_send()
-
-            return carry
-
-        lax.fori_loop(0, n_units, drain_units, 0)
+        rcopy(quarter_of(qo), quarter_of(qo), fw_send, fw_recv.at[0], (row, core_col)).wait_send()
+        rcopy(qs, qr, q_send, q_recv.at[0], (row, mid_col)).wait_send()
+        rcopy(out_hbm, out_hbm, o_send, o_recv, (row, pair_col)).wait_send()
+        pltpu.make_async_copy(out_hbm, out_hbm, l_sem).wait()
         v_core().wait_send()
 
     @pl.when(outer)
     def _():
-        def outputs(n, carry):
-            o_copy(2 * n).wait_recv()
-            return carry
-
-        lax.fori_loop(0, n_units // 2, outputs, 0)
+        rcopy(out_hbm, out_hbm, o_send, o_recv, (row, pair_col)).wait_recv()
         for core in range(2):
             for side in range(2):
                 v_pair(core, side).wait_send()
 
-    def drain_all(s, carry):
-        for j in range(2):
-            a_copy(s, j).wait_send()
-        b_copy(s).wait_send()
-        own_copy(s).wait_send()
-        return carry
-
-    lax.fori_loop(0, total, drain_all, 0)
+    for j in range(2):
+        rcopy(ra.at[:, :, j], ra.at[:, :, j], a_send.at[j], a_recv.at[0, j], (xn, col)).wait_send()
+    rcopy(rb, rb, b_send, b_recv.at[0], (yn, col)).wait_send()
+    rcopy(quarter_of(q), quarter_of(q), own_send, own_recv.at[0, 0], (row, own_col)).wait_send()
 
 
 def fused(integrals, occ_coef, virt_coef, pair_index):
@@ -401,16 +387,14 @@
     steps = -(-nus // STEP)
     padded = steps * STEP
     tail = padded - STEP
-    total = blocks * granules * steps
-    n_units = blocks * granules * GROUP
+    n_units = blocks * granules * (GROUP // 2)
     halves = GROUP // 2 * granules
 
     flipped = jnp.transpose(integrals, (1, 0, 2))
-    occ_rows = occ_coef.reshape(mus, rows, granules, GROUP).transpose(2, 1, 3, 0).reshape(occ, mus)
     spread = jnp.concatenate(
         [virt_coef[:tail], jnp.zeros((padded - nus, virt), BF16), virt_coef[tail:]], axis=0
     )
-    columns = spread.reshape(padded, cols // 2, 2, width).transpose(2, 1, 3, 0)
+    columns = spread.T.reshape(cols // 2, 2, width, padded)
 
     dma = pltpu.SemaphoreType.DMA
     r = padded * GROUP
@@ -434,19 +418,19 @@
             pltpu.VMEM((blocks, halves, 2, 2, width, LANES), BF16),
             pltpu.VMEM((STEP * GROUP, LANES), F32),
             dma((2,)),
-            dma((total, 2)), dma((total, 2)),
-            dma((total,)), dma((total,)),
-            dma((total,)), dma((2, total)),
-            dma((total,)), dma((total,)),
-            dma((n_units,)), dma((n_units,)),
-            dma((n_units // 2,)), dma((n_units // 2,)), dma((n_units // 2,)),
+            dma((2,)), dma((RING, 2)),
+            dma, dma((RING,)),
+            dma, dma((blocks * granules, 1 + -(-steps // BATCH))),
+            dma, dma((blocks * granules,)),
+            dma, dma((n_units,)),
+            dma, dma, dma,
             dma((4,)), dma((4, 2)), dma,
         ],
         compiler_params=pltpu.CompilerParams(
             collective_id=0, has_side_effects=True, vmem_limit_bytes=67043328
         ),
         name="half_transform",
-    )(flipped, occ_rows, columns)
+    )(flipped, occ_coef.T, columns)
     chosen = (lax.broadcasted_iota(jnp.int32, (n_pairs, n_pairs), 0) == pair_index[None, :]).astype(BF16)
     return jnp.einsum("iap,pk->iak", slab, chosen, preferred_element_type=F32).astype(BF16)
 
@@ -481,7 +465,7 @@
         rows == SIDES**2
         and cols == SIDES**3
         and integrals.shape[1] >= STEP
-        and integrals.shape[2] % LANES == 0
+        and integrals.shape[2] == 2 * LANES
         and occ_coef.shape[1] % (rows * GROUP) == 0
         and virt_coef.shape[1] % (cols * 16) == 0
     )

time: 311 us -> 222 us (0.71)
  Pallas kernels: 294 us -> 212 us
  local copies, waits for them, and re-layouts: 9.92 us -> 3.56 us
    pallas_call x1, Pallas kernels: 294 us -> 212 us  [fused(): pl.pallas_call(functools.partial(kernel, (nus, steps, blocks, granules)),...]
    reshape x3 -> x0, local copies, waits for them, and re-layouts: 9.84 us -> none  [the longest x2 8.18 us: fused(): columns = spread.reshape(padded, cols // 2, 2, width).transpose(2, 1, 3, 0)]
where the time goes in v1:
time: 222 us; the launch traced here: 221 us
  Pallas kernels  212 us (95%)
  matrix products  4.9 us (2%)
  local copies, waits for them, and re-layouts  3.56 us (2%)
    pallas_call x1, Pallas kernels, fused(): pl.pallas_call(functools.partial(kernel, (nus, steps, blocks, granules)),...  212 us
    dot_general x1, matrix products, fused(): jnp.einsum('iap,pk->iak', slab, chosen, preferred_element_type=F32)  4.9 us

profile of v1, /device:TPU:0, one launch (start us, length us, event | category | flops | bytes accessed | tf_op | source)
XLA Modules:
  0.0 221.2 jit_solution(4895007952811870363)
XLA Ops:
  0.0 0.0 slice-start
  0.0 0.0 slice-start.1
  0.0 0.1 pad.1.clone
  0.1 0.8 slice-done
  0.9 0.5 slice-done.1
  1.4 0.3 maximum_bitcast_fusion
  1.7 2.2 copy.5
  3.9 212.4 %half_transform.1 = bf16[24,288,256]{2,1,0:T(8,128)(2,1)} custom-call(bf16[300,600,256]{2,1,0:T(8,128)(2,1)} %bitcast.x_hbm, bf16[96,600]{1,0:T(8,128)(2,1)} %bitcast.10, bf16[4,2,288,304]{3,2,1,0:T(8,128)(2,1)} %bitcast.9), custom_call_target="tpu_custom_call" | custom-call | tf_op jit(solution)/shard_map/half_transform/pallas_call | solution.py:401
  216.3 4.9 %convolution_convert_fusion = bf16[24,288,256]{2,1,0:T(8,128)(2,1)} fusion(bf16[24,288,256]{2,1,0:T(8,128)(2,1)} %half_transform.1, s32[256]{0:T(256)} %param.7), kind=kOutput, calls=%fused_computation | convolution fusion | flops 907804672 | bytes 7078912 | tf_op jit(solution)/shard_map/iap,pk->iak/dot_general | solution.py:435
  (1 shorter events, 0.0 us)
Async XLA Ops:
  0.0 0.9 slice-start
  0.0 1.4 slice-start.1

commit v2 on v1

--- a/solution.py
+++ b/solution.py
@@ -19,6 +19,8 @@
 LAG_B = 8
 LAG_S = 1
 RING = 20
+V_FIRST = 28
+V_EVERY = 4
 BATCH = 4
 
 
@@ -151,6 +153,16 @@
             v_send.at[core * 2 + side], v_recv.at[q, side], (row, zp * 2 + core),
         )
 
+    def v_piece(n):
+        core, part_of = n // 4, n % 4
+        at = near + part_of // 2
+        rows_half = vt_hbm.shape[2] // 2
+        r = pl.ds(pl.multiple_of((part_of % 2) * rows_half, STEP), rows_half)
+        return rcopy(
+            vt_hbm.at[at, core, r], vr.at[q, at, r],
+            v_send.at[core * 2 + 1], v_recv.at[q, 1], (row, zp * 2 + core),
+        )
+
     def v_pair_arrival(core, side):
         start = far if side == 0 else near
         src = (zp % 2) * 2 + core
@@ -294,10 +306,11 @@
                 half[h, g * GROUP + i, pl.ds(at, STEP), :] = fsum[pl.ds(i, STEP, stride=GROUP), :].astype(BF16)
             own_copy(s2).start()
 
-        @pl.when(outer & (t == steps + LAG_B))
-        def _():
-            v_pair(0, 1).start()
-            v_pair(1, 1).start()
+        tv = t - V_FIRST
+
+        @pl.when(outer & (tv >= 0) & (tv % V_EVERY == 0) & (tv // V_EVERY < 8))
+        def _():
+            v_piece(tv // V_EVERY).start()
 
         tf = t - lag_f
         gf, uf = tf // steps, tf % steps
@@ -467,7 +480,8 @@
         and integrals.shape[1] >= STEP
         and integrals.shape[2] == 2 * LANES
         and occ_coef.shape[1] % (rows * GROUP) == 0
-        and virt_coef.shape[1] % (cols * 16) == 0
+        and virt_coef.shape[1] % (cols * 2 * STEP) == 0
+        and occ_coef.shape[1] // (rows * GROUP) * 2 * (integrals.shape[1] // STEP) > V_FIRST + 8 * V_EVERY
     )
     form = fused if fits else plain
     return form(integrals, occ_coef, virt_coef, pair_index)

time: 222 us -> 215 us (0.968)
  Pallas kernels: 212 us -> 205 us
    pallas_call x1, Pallas kernels: 212 us -> 205 us  [fused(): pl.pallas_call(functools.partial(kernel, (nus, steps, blocks, granules)),...]
where the time goes in v2:
time: 215 us; the launch traced here: 214 us
  Pallas kernels  205 us (95%)
  matrix products  4.9 us (2%)
  local copies, waits for them, and re-layouts  3.56 us (2%)
    pallas_call x1, Pallas kernels, fused(): pl.pallas_call(functools.partial(kernel, (nus, steps, blocks, granules)),...  205 us
    dot_general x1, matrix products, fused(): jnp.einsum('iap,pk->iak', slab, chosen, preferred_element_type=F32)  4.9 us

profile of v2, /device:TPU:0, one launch (start us, length us, event | category | flops | bytes accessed | tf_op | source)
XLA Modules:
  0.0 214.2 jit_solution(8614096942763399873)
XLA Ops:
  0.0 0.0 slice-start
  0.0 0.0 slice-start.1
  0.0 0.1 pad.1.clone
  0.1 0.8 slice-done
  0.9 0.5 slice-done.1
  1.4 0.3 maximum_bitcast_fusion
  1.7 2.2 %copy.5 = bf16[2304,304]{1,0:T(8,128)(2,1)} copy(bf16[2304,304]{0,1:T(8,128)(2,1)S(1)} %maximum_bitcast_fusion) | data formatting | bytes 2801664 | tf_op jit(solution)/shard_map/transpose | solution.py:410
  3.9 205.4 %half_transform.1 = bf16[24,288,256]{2,1,0:T(8,128)(2,1)} custom-call(bf16[300,600,256]{2,1,0:T(8,128)(2,1)} %bitcast.x_hbm, bf16[96,600]{1,0:T(8,128)(2,1)} %bitcast.10, bf16[4,2,288,304]{3,2,1,0:T(8,128)(2,1)} %bitcast.9), custom_call_target="tpu_custom_call" | custom-call | tf_op jit(solution)/shard_map/half_transform/pallas_call | solution.py:414
  209.3 4.9 %convolution_convert_fusion = bf16[24,288,256]{2,1,0:T(8,128)(2,1)} fusion(bf16[24,288,256]{2,1,0:T(8,128)(2,1)} %half_transform.1, s32[256]{0:T(256)} %param.7), kind=kOutput, calls=%fused_computation | convolution fusion | flops 907804672 | bytes 7078912 | tf_op jit(solution)/shard_map/iap,pk->iak/dot_general | solution.py:448
  (1 shorter events, 0.0 us)
Async XLA Ops:
  0.0 0.9 slice-start
  0.0 1.4 slice-start.1
